TPU v7x, 128 devices: a whole 4x4x4 slice. The times are simulated.
128 devices in a mesh: wide: 8 (over y_lo, z), narrow: 16 (over y_hi, x, core).
Axes of the slice: x: 4, y: 4 (y_hi: 2, y_lo: 2; y = y_hi * 2 + y_lo), z: 4, core: 2. Of those that a mesh axis runs over, the one named last changes fastest.
Arguments:
- saved_inputs: bfloat16 [2048, 5120], P('wide', 'narrow'), may hold values from -6 to 6
- out_grads: bfloat16 [2048, 5120], P('wide', 'narrow'), may hold values from -48 to 48
- seq_ids: int32 [2048], P('wide'), may hold values from 0 to 15, as said below
- seq_counts: int32 [16], P('wide'), may hold values from 64 to 192, as said below
- basis_in: bfloat16 [5120, 5120], P('narrow'), may hold values from -0.078125 to 0.078125
- basis_out: bfloat16 [5120, 5120], P('narrow'), may hold values from -0.078125 to 0.078125
- query_rotated: bfloat16 [5120, 5120], P('narrow', 'wide'), may hold values from -6 to 6
- damping: float32 [], replicated, may hold values from 0.05 to 0.5
Outputs:
- eigenvalues: float32 [5120, 5120], P('narrow', 'wide')
- preconditioned: float32 [5120, 5120], P('narrow', 'wide')
Inputs may be any that keep to these rules, and one draw needn't show every extreme that they name: seq_ids names for each token its sequence; the 256 tokens of block w of the token axis belong to the sequences 2 * w to 2 * w + 1, each having at least one token. seq_counts[s] is the number of tokens whose seq_ids equal s.
All inputs are finite; a program needn't handle non-finite values.
Results may differ from a plain program's by a relative error of at most 0.01.
Values may be sent and summed in bfloat16 or wider, within the bound.
A program may use at most 128 MiB of HBM per device.

v0:
```python
import jax
import jax.numpy as jnp
from jax import lax
from jax.sharding import PartitionSpec as P


def in_order(pieces, dim):
    pieces = jnp.moveaxis(pieces, 0, dim)
    shape = pieces.shape
    return pieces.reshape(*shape[:dim], shape[dim] * shape[dim + 1], *shape[dim + 2 :])


def copy_for_each(value, axis):
    copies = jnp.broadcast_to(value, (lax.axis_size(axis), *value.shape))
    return lax.all_to_all(copies, axis, split_axis=0, concat_axis=0, tiled=True)


def collect(value, axis, dim):
    return in_order(copy_for_each(value, axis), dim)


def in_one_piece(arrays, axis, dim, along):
    widths = [a.shape[along] for a in arrays]
    both = jnp.concatenate(arrays, axis=along)
    whole = lax.all_gather(both, axis, axis=dim, tiled=True)
    return tuple(jnp.split(whole, [sum(widths[:k]) for k in range(1, len(widths))], axis=along))


def shards(
    saved_inputs, out_grads, seq_ids, seq_counts, basis_in, basis_out, query_rotated, damping
):
    part_in = jnp.dot(saved_inputs, basis_in, preferred_element_type=jnp.float32)
    part_grad = jnp.dot(out_grads, basis_out, preferred_element_type=jnp.float32)
    rot_in = lax.psum(part_in, "narrow").astype(jnp.bfloat16)
    rot_grad = lax.psum_scatter(part_grad, "narrow", scatter_dimension=1, tiled=True).astype(
        jnp.bfloat16
    )
    seq_local = seq_counts.shape[0]
    tok_local = seq_ids.shape[0]
    offset = lax.axis_index("wide") * seq_local
    member = seq_ids[None, :] - offset == jnp.arange(seq_local, dtype=jnp.int32)[:, None]
    weight = (
        jnp.where(member, 1.0, 0.0).astype(jnp.float32) / seq_counts.astype(jnp.float32)[:, None]
    )
    weighted = (rot_grad.astype(jnp.float32)[None, :, :] * weight[:, :, None]).astype(jnp.bfloat16)
    total_seqs = seq_local * lax.axis_size("wide")
    groups = lax.axis_size("wide")
    all_weighted = collect(weighted, "wide", 0)
    all_weighted = all_weighted.reshape(groups, seq_local, tok_local, all_weighted.shape[2])
    column_rows = lax.all_to_all(rot_in, "wide", split_axis=1, concat_axis=0, tiled=True)
    column_rows = column_rows.reshape(groups, tok_local, column_rows.shape[1])
    per_seq = jnp.einsum(
        "gsti,gtj->gsij", all_weighted, column_rows, preferred_element_type=jnp.float32
    )
    eigenvalues = jnp.sum(per_seq * per_seq, axis=(0, 1)) / total_seqs
    scaled = (query_rotated.astype(jnp.float32) / (eigenvalues + damping)).astype(jnp.bfloat16)
    width = query_rotated.shape[1]
    in_columns = lax.dynamic_slice_in_dim(basis_in, lax.axis_index("wide") * width, width, 1)
    all_scaled, all_columns = in_one_piece((scaled, in_columns), "narrow", 0, 1)
    middle = jnp.dot(basis_out, all_scaled, preferred_element_type=jnp.float32).astype(jnp.bfloat16)
    partial_back = lax.dot_general(
        middle, all_columns, (((1,), (1,)), ((), ())), preferred_element_type=jnp.float32
    )
    preconditioned = lax.psum_scatter(partial_back, "wide", scatter_dimension=1, tiled=True)
    return (eigenvalues, preconditioned)


def solution(mesh):
    return jax.shard_map(
        shards,
        mesh=mesh,
        in_specs=(
            P("wide", "narrow"),
            P("wide", "narrow"),
            P("wide"),
            P("wide"),
            P("narrow", None),
            P("narrow", None),
            P("narrow", "wide"),
            P(),
        ),
        out_specs=(P("narrow", "wide"), P("narrow", "wide")),
        check_vma=False,
    )
```

profile of v0, /device:TPU:1, one launch (start us, length us, event | category | flops | bytes accessed | tf_op | source)
XLA Modules:
  0.0 396.9 jit_solution(1464753406761184582)
XLA Ops:
  7.2 0.0 copy-start
  7.2 0.0 reduce-scatter.3.cloned.1.call-start
  7.2 1.9 copy-done
  9.1 5.0 %fusion.11 = f32[256,5120]{0,1:T(8,128)} fusion(bf16[256,320]{0,1:T(8,128)(2,1)} %param.9, bf16[320,5120]{1,0:T(8,128)(2,1)S(1)} %copy-done), kind=kOutput, calls=%fused_computation.17 | convolution fusion | flops 838860800 | bytes 8683520 | tf_op jit(solution)/shard_map/dot_general | solution.py:33
  14.1 0.0 copy-start.3
  14.1 0.0 reduce-scatter.3.cloned.1.call-update
  14.2 0.9 copy-done.3
  15.0 5.8 %fusion.12 = f32[256,5120]{1,0:T(8,128)} fusion(bf16[256,320]{0,1:T(8,128)(2,1)S(1)} %copy-done.3, bf16[320,5120]{1,0:T(8,128)(2,1)} %param.12), kind=kOutput, calls=%fused_computation.18 | convolution fusion | flops 838860800 | bytes 8683520 | tf_op jit(solution)/shard_map/dot_general | solution.py:32
  20.9 100.9 %all-reduce.1 = bf16[256,5120]{1,0:T(8,128)(2,1)} all-reduce(f32[256,5120]{1,0:T(8,128)} %fusion.12), channel_id=1, replica_groups=mesh['wide'=8,'narrow'=16] {'narrow'}, use_global_device_ids=true, to_apply=%region_1.0 | all-reduce | flops 1310720 | bytes 7864320 | tf_op jit(solution)/shard_map/psum | solution.py:34
  121.8 3.5 copy.14
  125.3 0.0 copy-start.5
  125.3 0.0 copy-start.4
  125.3 9.7 %all-to-all-start.1 = ((bf16[256,8,640]{2,0,1:T(8,128)(2,1)}), bf16[256,8,640]{2,0,1:T(8,128)(2,1)}, u32[]{:S(2)}, u32[]{:S(2)}) async-start(bf16[256,8,640]{2,0,1:T(8,128)(2,1)} %bitcast.17), calls=%async_computation.2 | async-start | bytes 5242880 | tf_op jit(solution)/shard_map/all_to_all | solution.py:50
  135.0 0.0 copy-done.5
  135.0 0.0 copy-done.4
  135.1 0.1 fusion.10
  135.1 0.0 reduce-scatter.3.cloned.1.call-done
  135.1 1.0 convert_convert_fusion
  136.1 0.8 multiply_convert_fusion
  136.9 30.0 %all-to-all-done.1 = bf16[256,8,640]{2,0,1:T(8,128)(2,1)} async-done(((bf16[256,8,640]{2,0,1:T(8,128)(2,1)}), bf16[256,8,640]{2,0,1:T(8,128)(2,1)}, u32[]{:S(2)}, u32[]{:S(2)}) %all-to-all-start.1) | async-done | bytes 2621472 | tf_op jit(solution)/shard_map/all_to_all | solution.py:50
  167.0 2.7 broadcast_in_dim.18
  169.7 4.4 %all-to-all-start = ((bf16[8,2,256,320]{2,3,1,0:T(8,128)(2,1)}), bf16[8,2,256,320]{2,3,1,0:T(8,128)(2,1)}, u32[]{:S(2)}, u32[]{:S(2)}) async-start(bf16[8,2,256,320]{2,3,1,0:T(8,128)(2,1)} %broadcast_in_dim.18), calls=%async_computation.1 | async-start | bytes 5242880 | tf_op jit(solution)/shard_map/all_to_all | solution.py:15
  174.1 0.0 all-gather.2.cloned.1.call-start
  174.8 1.8 constant_dynamic-slice_fusion
  176.6 29.3 %all-to-all-done = bf16[8,2,256,320]{2,3,1,0:T(8,128)(2,1)} async-done(((bf16[8,2,256,320]{2,3,1,0:T(8,128)(2,1)}), bf16[8,2,256,320]{2,3,1,0:T(8,128)(2,1)}, u32[]{:S(2)}, u32[]{:S(2)}) %all-to-all-start) | async-done | bytes 2621472 | tf_op jit(solution)/shard_map/all_to_all | solution.py:15
  205.9 0.0 copy-start.2
  205.9 0.0 copy-start.1
  205.9 4.9 %multiply_reduce_fusion = f32[320,640]{1,0:T(8,128)S(1)} fusion(bf16[8,2,256,320]{2,3,1,0:T(8,128)(2,1)} %all-to-all-done, bf16[256,8,640]{2,0,1:T(8,128)(2,1)} %all-to-all-done.1), kind=kOutput, calls=%fused_computation | convolution fusion | flops 1684070400 | bytes 6062080 | tf_op jit(solution)/shard_map/gsti,gtj->gsij/dot_general | solution.py:52
  210.8 0.0 copy-done.2
  210.8 1.0 divide_convert_fusion
  211.8 0.0 copy-done.1
  211.8 1.0 pad_maximum_fusion
  212.8 0.0 all-gather.2.cloned.1.call-update
  212.8 0.2 reduce-scatter.5.cloned.1.call-start
  213.0 90.6 %all-gather.2.cloned.1.call-done = bf16[5120,1280]{1,0:T(8,128)(2,1)} async-done(((bf16[320,1280]{1,0:T(8,128)(2,1)}), bf16[5120,1280]{1,0:T(8,128)(2,1)}) %all-gather.2.cloned.1.call-update) | async-done | bytes 13107216 | tf_op jit(solution)/shard_map/all_gather | solution.py:25
  303.6 13.7 %fusion = f32[320,5120]{1,0:T(8,128)} fusion(bf16[5120,1280]{1,0:T(8,128)(2,1)} %all-gather.2.cloned.1.call-done, bf16[320,5120]{1,0:T(8,128)(2,1)S(1)} %copy-done), kind=kOutput, calls=%fused_computation.1 | convolution fusion | flops 4194508800 | bytes 22937600 | tf_op jit(solution)/shard_map/dot_general | solution.py:61
  317.3 0.0 reduce-scatter.5.cloned.1.call-update
  317.3 73.1 %reduce-scatter.5.cloned.1.call-done = f32[320,640]{1,0:T(8,128)} async-done(((f32[320,5120]{1,0:T(8,128)}), f32[320,640]{1,0:T(8,128)}) %reduce-scatter.5.cloned.1.call-update) | async-done | bytes 819216 | tf_op jit(solution)/shard_map/reduce_scatter | solution.py:64
  (2 shorter events, 0.0 us)
Async XLA Ops:
  7.2 1.9 copy-start
  7.2 128.0 %reduce-scatter.3.cloned.1.call-start = ((), (), s32[]{:S(2)}) async-start(), calls=%async_computation.4 | async-start | bytes 5570560 | tf_op jit(solution)/shard_map/reduce_scatter | solution.py:35
  14.1 0.9 copy-start.3
  125.3 9.7 %copy-start.5 = (s32[2]{0:T(128)S(1)}, s32[2]{0:T(128)}, u32[]{:S(2)}) copy-start(s32[2]{0:T(128)} %param.11) | copy-start | bytes 28
  125.3 9.7 %copy-start.4 = (s32[256]{0:T(256)S(1)}, s32[256]{0:T(256)}, u32[]{:S(2)}) copy-start(s32[256]{0:T(256)} %param.10) | copy-start | bytes 3076
  125.3 41.6 %all-to-all-start.1 = ((bf16[256,8,640]{2,0,1:T(8,128)(2,1)}), bf16[256,8,640]{2,0,1:T(8,128)(2,1)}, u32[]{:S(2)}, u32[]{:S(2)}) async-start(bf16[256,8,640]{2,0,1:T(8,128)(2,1)} %bitcast.17), calls=%async_computation.2 | async-start | bytes 5242880 | tf_op jit(solution)/shard_map/all_to_all | solution.py:50
  169.7 36.2 %all-to-all-start = ((bf16[8,2,256,320]{2,3,1,0:T(8,128)(2,1)}), bf16[8,2,256,320]{2,3,1,0:T(8,128)(2,1)}, u32[]{:S(2)}, u32[]{:S(2)}) async-start(bf16[8,2,256,320]{2,3,1,0:T(8,128)(2,1)} %broadcast_in_dim.18), calls=%async_computation.1 | async-start | bytes 5242880 | tf_op jit(solution)/shard_map/all_to_all | solution.py:15
  174.1 129.5 %all-gather.2.cloned.1.call-start = ((), (), s32[]{:S(2)}) async-start(), calls=%async_computation.5 | async-start | bytes 13926400 | tf_op jit(solution)/shard_map/all_gather | solution.py:25
  205.9 4.9 %copy-start.2 = (bf16[320,640]{1,0:T(8,128)(2,1)S(1)}, bf16[320,640]{1,0:T(8,128)(2,1)}, u32[]{:S(2)}) copy-start(bf16[320,640]{1,0:T(8,128)(2,1)} %param.14) | copy-start | bytes 1228804
  205.9 5.9 %copy-start.1 = (bf16[320,640]{1,0:T(8,128)(2,1)S(1)}, bf16[320,640]{1,0:T(8,128)(2,1)}, u32[]{:S(2)}) copy-start(bf16[320,640]{1,0:T(8,128)(2,1)} %constant_dynamic-slice_fusion) | copy-start | bytes 1228804
  212.8 177.5 %reduce-scatter.5.cloned.1.call-start = ((), (), s32[]{:S(2)}) async-start(), calls=%async_computation.6 | async-start | bytes 7372800 | tf_op jit(solution)/shard_map/reduce_scatter | solution.py:64
Sparse Core Ops, SparseCore 0:
  14.3 107.6 reduce-scatter.2
  212.9 90.6 all-gather.1
  317.4 72.8 reduce-scatter.4
where the time goes:
time: 397 us
  waiting for transfers between devices  223 us (56%)
  blocking collectives  101 us (25%)
  matrix products  29.4 us (7%)
  between operations  14.5 us (4%)
  starting transfers between devices  14.4 us (4%)
  local copies, waits for them, and re-layouts  10.9 us (3%)
    psum x1, blocking collectives, shards(): rot_in = lax.psum(part_in, 'narrow').astype(jnp.bfloat16)  101 us
    all_gather x1, waiting for transfers between devices, in_one_piece(): whole = lax.all_gather(both, axis, axis=dim, tiled=True)  90.6 us
    reduce_scatter x1, waiting for transfers between devices, shards(): lax.psum_scatter(partial_back, 'wide', scatter_dimension=1, tiled=True)  73.1 us
    all_to_all x1, waiting for transfers between devices, shards(): lax.all_to_all(rot_in, 'wide', split_axis=1, concat_axis=0, tiled=True)  30 us
    all_to_all x1, waiting for transfers between devices, copy_for_each(): return lax.all_to_all(copies, axis, split_axis=0, concat_axis=0, tiled=True)  29.3 us
    dot_general x1, matrix products, shards(): lax.dot_general(middle, all_columns, (((1,), (1,)), ((), ())), preferred_...  13.7 us
    all_to_all x1, starting transfers between devices, shards(): lax.all_to_all(rot_in, 'wide', split_axis=1, concat_axis=0, tiled=True)  9.72 us
  transfers between devices with their start and end apart: 5, of which 4 were waited for; matrix products, arithmetic and copies ran while one was open for 3% of the time, Pallas kernels for 0%

commit v1 on v0

--- a/solution.py
+++ b/solution.py
@@ -31,7 +31,7 @@
 ):
     part_in = jnp.dot(saved_inputs, basis_in, preferred_element_type=jnp.float32)
     part_grad = jnp.dot(out_grads, basis_out, preferred_element_type=jnp.float32)
-    rot_in = lax.psum(part_in, "narrow").astype(jnp.bfloat16)
+    rot_in = jnp.sum(lax.all_gather(part_in, "narrow"), axis=0).astype(jnp.bfloat16)
     rot_grad = lax.psum_scatter(part_grad, "narrow", scatter_dimension=1, tiled=True).astype(
         jnp.bfloat16
     )

time: 397 us -> 804 us (2.03)
  waiting for transfers between devices: 223 us -> 703 us
  blocking collectives: 101 us -> 0 us
  other arithmetic: 3.84 us -> 30.9 us
    all_gather x0 -> x1, waiting for transfers between devices: none -> 431 us  [shards(): lax.all_gather(part_in, 'narrow')]
    psum x1 -> x0, blocking collectives: 101 us -> none  [shards(): rot_in = lax.psum(part_in, 'narrow').astype(jnp.bfloat16)]
    reduce_scatter x1, waiting for transfers between devices: 0.01 us -> 79.5 us  [shards(): lax.psum_scatter(part_grad, 'narrow', scatter_dimension=1, tiled=True)]
    all_to_all x1, waiting for transfers between devices: 29.3 us -> 0.01 us  [copy_for_each(): return lax.all_to_all(copies, axis, split_axis=0, concat_axis=0, tiled=True)]
    reduce_sum x0 -> x1, other arithmetic: none -> 27.8 us  [shards(): jnp.sum(lax.all_gather(part_in, 'narrow'), axis=0).astype(jnp.bfloat16)]
    convert_element_type x0 -> x2, local copies, waits for them, and re-layouts: none -> 8.76 us  [shards(): jnp.sum(lax.all_gather(part_in, 'narrow'), axis=0).astype(jnp.bfloat16)]
  transfers between devices with their start and end apart: 5 -> 6, of which waited for: 4 -> 5; matrix products, arithmetic and copies ran while one was open for 3% -> 6% of each run, Pallas kernels for 0% -> 0%
where the time goes in v1:
time: 804 us; the launch traced here: 803 us
  waiting for transfers between devices  703 us (87%)
  other arithmetic  30.9 us (4%)
  matrix products  29.8 us (4%)
  local copies, waits for them, and re-layouts  15.7 us (2%)
  between operations  14.5 us (2%)
  starting transfers between devices  9.17 us (1%)
    all_gather x1, waiting for transfers between devices, shards(): lax.all_gather(part_in, 'narrow')  431 us
    all_gather x1, waiting for transfers between devices, in_one_piece(): whole = lax.all_gather(both, axis, axis=dim, tiled=True)  89.9 us
    reduce_scatter x1, waiting for transfers between devices, shards(): lax.psum_scatter(part_grad, 'narrow', scatter_dimension=1, tiled=True)  79.5 us
    reduce_scatter x1, waiting for transfers between devices, shards(): lax.psum_scatter(partial_back, 'wide', scatter_dimension=1, tiled=True)  73.1 us
    all_to_all x1, waiting for transfers between devices, shards(): lax.all_to_all(rot_in, 'wide', split_axis=1, concat_axis=0, tiled=True)  29.4 us
    reduce_sum x1, other arithmetic, shards(): jnp.sum(lax.all_gather(part_in, 'narrow'), axis=0).astype(jnp.bfloat16)  27.8 us
  transfers between devices with their start and end apart: 6, of which 5 were waited for; matrix products, arithmetic and copies ran while one was open for 6% of the time, Pallas kernels for 0%

profile of v1, /device:TPU:1, one launch (start us, length us, event | category | flops | bytes accessed | tf_op | source)
XLA Modules:
  0.0 803.3 jit_solution(12637595323661226069)
XLA Ops:
  7.2 0.0 copy-start
  7.2 0.0 reduce-scatter.3.cloned.1.call-start
  7.2 1.9 copy-done
  9.1 5.0 fusion.11
  14.1 0.0 copy-start.3
  14.1 0.0 reduce-scatter.3.cloned.1.call-update
  14.2 0.0 all-gather.6.cloned.1.call-start
  14.2 0.8 copy-done.3
  15.0 5.8 fusion.12
  20.8 0.0 copy-start.5
  20.8 0.0 copy-start.4
  20.9 0.0 all-gather.6.cloned.1.call-update
  20.9 0.6 copy-done.5
  21.5 0.0 copy-done.4
  21.5 0.1 fusion.10
  21.6 79.5 %reduce-scatter.3.cloned.1.call-done = f32[256,320]{0,1:T(8,128)} async-done(((f32[256,5120]{0,1:T(8,128)}), f32[256,320]{0,1:T(8,128)}) %reduce-scatter.3.cloned.1.call-update) | async-done | bytes 327696 | tf_op jit(solution)/shard_map/reduce_scatter | solution.py:35
  101.1 1.0 convert_convert_fusion
  102.2 1.8 broadcast_in_dim.18
  103.9 4.4 all-to-all-start
  108.4 431.4 %all-gather.6.cloned.1.call-done = f32[4096,5120]{1,0:T(8,128)} async-done(((f32[256,5120]{1,0:T(8,128)}), f32[4096,5120]{1,0:T(8,128)}) %all-gather.6.cloned.1.call-update) | async-done | bytes 83886096 | tf_op jit(solution)/shard_map/all_gather | solution.py:34
  539.7 27.8 %reduce_sum.18 = bf16[256,5120]{1,0:T(8,128)(2,1)} reduce(f32[16,256,5120]{2,1,0:T(8,128)} %bitcast, f32[]{:T(128)} %constant.7.clone.1), dimensions={0}, to_apply=%region_1.0 | reduce | flops 19660800 | bytes 86507520 | tf_op jit(solution)/shard_map/reduce_sum | solution.py:34
  567.5 4.4 copy.11
  571.9 4.4 copy.12
  576.3 0.0 all-to-all-done
  576.3 4.4 all-to-all-start.1
  580.7 0.0 all-gather.4.cloned.1.call-start
  581.4 1.8 constant_dynamic-slice_fusion
  583.2 29.4 %all-to-all-done.1 = bf16[256,8,640]{2,0,1:T(8,128)(2,1)} async-done(((bf16[256,8,640]{2,0,1:T(8,128)(2,1)}), bf16[256,8,640]{2,0,1:T(8,128)(2,1)}, u32[]{:S(2)}, u32[]{:S(2)}) %all-to-all-start.1) | async-done | bytes 2621472 | tf_op jit(solution)/shard_map/all_to_all | solution.py:50
  612.6 0.0 copy-start.2
  612.6 0.0 copy-start.1
  612.6 4.9 multiply_reduce_fusion
  617.4 0.0 copy-done.2
  617.5 1.0 divide_convert_fusion
  618.5 0.0 copy-done.1
  618.5 1.0 pad_maximum_fusion
  619.4 0.0 all-gather.4.cloned.1.call-update
  619.5 0.2 reduce-scatter.5.cloned.1.call-start
  619.7 89.9 %all-gather.4.cloned.1.call-done = bf16[5120,1280]{1,0:T(8,128)(2,1)} async-done(((bf16[320,1280]{1,0:T(8,128)(2,1)}), bf16[5120,1280]{1,0:T(8,128)(2,1)}) %all-gather.4.cloned.1.call-update) | async-done | bytes 13107216 | tf_op jit(solution)/shard_map/all_gather | solution.py:25
  709.6 14.1 %fusion = f32[320,5120]{1,0:T(8,128)} fusion(bf16[5120,1280]{1,0:T(8,128)(2,1)} %all-gather.4.cloned.1.call-done, bf16[320,5120]{1,0:T(8,128)(2,1)S(1)} %copy-done), kind=kOutput, calls=%fused_computation.1 | convolution fusion | flops 4194508800 | bytes 22937600 | tf_op jit(solution)/shard_map/dot_general | solution.py:61
  723.7 0.0 reduce-scatter.5.cloned.1.call-update
  723.7 73.1 %reduce-scatter.5.cloned.1.call-done = f32[320,640]{1,0:T(8,128)} async-done(((f32[320,5120]{1,0:T(8,128)}), f32[320,640]{1,0:T(8,128)}) %reduce-scatter.5.cloned.1.call-update) | async-done | bytes 819216 | tf_op jit(solution)/shard_map/reduce_scatter | solution.py:64
  (3 shorter events, 0.1 us)
Async XLA Ops:
  7.2 1.9 copy-start
  7.2 93.9 %reduce-scatter.3.cloned.1.call-start = ((), (), s32[]{:S(2)}) async-start(), calls=%async_computation.4 | async-start | bytes 5570560 | tf_op jit(solution)/shard_map/reduce_scatter | solution.py:35
  14.1 0.9 copy-start.3
  14.2 525.6 %all-gather.6.cloned.1.call-start = ((), (), s32[]{:S(2)}) async-start(), calls=%async_computation.7 | async-start | bytes 89128960 | tf_op jit(solution)/shard_map/all_gather | solution.py:34
  20.8 0.7 copy-start.5
  20.8 0.7 copy-start.4
  103.9 472.3 %all-to-all-start = ((bf16[8,2,256,320]{2,3,1,0:T(8,128)(2,1)}), bf16[8,2,256,320]{2,3,1,0:T(8,128)(2,1)}, u32[]{:S(2)}, u32[]{:S(2)}) async-start(bf16[8,2,256,320]{2,3,1,0:T(8,128)(2,1)} %broadcast_in_dim.18), calls=%async_computation.1 | async-start | bytes 5242880 | tf_op jit(solution)/shard_map/all_to_all | solution.py:15
  576.3 36.3 %all-to-all-start.1 = ((bf16[256,8,640]{2,0,1:T(8,128)(2,1)}), bf16[256,8,640]{2,0,1:T(8,128)(2,1)}, u32[]{:S(2)}, u32[]{:S(2)}) async-start(bf16[256,8,640]{2,0,1:T(8,128)(2,1)} %copy.12), calls=%async_computation.2 | async-start | bytes 5242880 | tf_op jit(solution)/shard_map/all_to_all | solution.py:50
  580.7 128.9 %all-gather.4.cloned.1.call-start = ((), (), s32[]{:S(2)}) async-start(), calls=%async_computation.5 | async-start | bytes 13926400 | tf_op jit(solution)/shard_map/all_gather | solution.py:25
  612.6 4.9 copy-start.2
  612.6 5.9 copy-start.1
  619.5 177.3 %reduce-scatter.5.cloned.1.call-start = ((), (), s32[]{:S(2)}) async-start(), calls=%async_computation.6 | async-start | bytes 7372800 | tf_op jit(solution)/shard_map/reduce_scatter | solution.py:64
Sparse Core Ops, SparseCore 0:
  14.3 86.8 reduce-scatter.2
  103.6 436.0 all-gather.5
  619.6 89.9 all-gather.3
  723.8 72.8 reduce-scatter.4
